TPU v7x, 32 devices: a whole 2x2x4 slice. The times are simulated.
32 devices in a mesh: replica: 2 (over x), tp: 16 (over z, y, core).
Axes of the slice: x: 2, y: 2, z: 4, core: 2. Of those that a mesh axis runs over, the one named last changes fastest.
Arguments:
- hidden_in: bfloat16 [8, 16384], P('replica', 'tp'), parts along dimension 0, may hold values from -60 to 60
- norm_gain: bfloat16 [16384], P('tp'), may hold values from 0.5 to 1.5
- w_qkv: bfloat16 [16384, 9216], P(None, 'tp'), may hold values from -0.046875 to 0.046875
- w_out: bfloat16 [8192, 16384], P('tp'), may hold values from -0.09375 to 0.09375
- key_cache: bfloat16 [8, 2048, 512], P('replica', 'tp'), parts along dimension 0, may hold values from -1200 to 1200
- value_cache: bfloat16 [8, 2048, 512], P('replica', 'tp'), parts along dimension 0, may hold values from -6 to 6
- lengths: int32 [8], P('replica'), parts along dimension 0, may hold values from 1024 to 2048
- positions: int32 [8], P('replica'), parts along dimension 0, may hold values from 0 to 4095
Outputs:
- attn_out: bfloat16 [8, 16384], P('replica', 'tp'), parts along dimension 0
- token_scale: float32 [8], P('replica'), parts along dimension 0
There are 2 independent parts, one for each index of `replica`. A program takes and returns all parts, laid end to end along the dimension named above; an argument that names none is the same for every part. Nothing has to cross between parts.
All inputs are finite; a program needn't handle non-finite values.
Results may differ from a plain program's by a relative error of at most 0.017.
The roundings to bfloat16 on the way count: a program that leaves them out, or rounds other values in their place, can miss the bound.
Values may be sent and summed in bfloat16 or wider, within the bound.
A program may use at most 128 MiB of HBM per device.

v0:
```python
import jax
import jax.numpy as jnp
from jax import lax
from jax.sharding import PartitionSpec as P

QUERY_HEADS = 64
KEY_VALUE_HEADS = 4
HEAD_SIZE = 128


def combined_all(value, axis, join):
    pieces = jax.tree.map(lambda part: lax.all_gather(part, axis), value)
    head = jax.tree.map(lambda part: part[0], pieces)
    tail = jax.tree.map(lambda part: part[1:], pieces)
    total, _ = lax.scan(lambda total, slab: (join(total, slab), None), head, tail)
    return total


def apply_rotation(heads, positions):
    half = HEAD_SIZE // 2
    freq = 500000.0 ** (-(jnp.arange(half, dtype=jnp.float32) * 2.0) / HEAD_SIZE)
    angle = positions.astype(jnp.float32)[:, None] * freq[None, :]
    cosine = jnp.cos(angle)[:, None, :]
    sine = jnp.sin(angle)[:, None, :]
    leading_part = heads[..., :half]
    second = heads[..., half:]
    return jnp.concatenate(
        [leading_part * cosine - second * sine, second * cosine + leading_part * sine], axis=-1
    )


def join_stats(left, right):
    return (left[0] + right[0], jnp.maximum(left[1], right[1]))


def join_parts(left, right):
    top = jnp.maximum(left[0], right[0])
    scale_left = jnp.exp(left[0] - top)
    scale_right = jnp.exp(right[0] - top)
    total = left[1] * scale_left + right[1] * scale_right
    summed = left[2] * scale_left[..., None] + right[2] * scale_right[..., None]
    return (top, total, summed)


def on_device(hidden_in, norm_gain, w_qkv, w_out, key_cache, value_cache, lengths, positions):
    batch_count = hidden_in.shape[0]
    width = w_qkv.shape[0]
    position_range = key_cache.shape[1]
    group_count = QUERY_HEADS // KEY_VALUE_HEADS
    query_width = QUERY_HEADS * HEAD_SIZE
    key_width = KEY_VALUE_HEADS * HEAD_SIZE
    own_heads = w_out.shape[0] // HEAD_SIZE
    inv = 1.0 / HEAD_SIZE**0.5
    values = hidden_in.astype(jnp.float32)
    gained = values * norm_gain.astype(jnp.float32)[None, :]
    squares, gained_peak = combined_all(
        (jnp.sum(values * values, axis=-1), jnp.max(jnp.abs(gained), axis=-1)), "tp", join_stats
    )
    rstd = lax.rsqrt(squares / width + 1e-05)
    normed = gained * rstd[:, None]
    peak = gained_peak * rstd
    token_scale = (peak + 1e-06) / 448.0
    quant = (normed / token_scale[:, None]).astype(jnp.bfloat16)
    local_proj = jnp.dot(
        lax.all_gather(quant, "tp", axis=1, tiled=True), w_qkv, preferred_element_type=jnp.float32
    )
    local_proj = (local_proj * token_scale[:, None]).astype(jnp.bfloat16)
    query_key_value = lax.all_gather(local_proj, "tp", axis=1, tiled=True)
    query_rows = apply_rotation(
        query_key_value[:, :query_width]
        .astype(jnp.float32)
        .reshape(batch_count, QUERY_HEADS, HEAD_SIZE),
        positions,
    ).astype(jnp.bfloat16)
    latest_key = apply_rotation(
        query_key_value[:, query_width : query_width + key_width]
        .astype(jnp.float32)
        .reshape(batch_count, KEY_VALUE_HEADS, HEAD_SIZE),
        positions,
    )
    latest_value = (
        query_key_value[:, query_width + key_width :]
        .astype(jnp.float32)
        .reshape(batch_count, KEY_VALUE_HEADS, HEAD_SIZE)
    )
    grouped_query = query_rows.reshape(batch_count, KEY_VALUE_HEADS, group_count, HEAD_SIZE)
    key_rows = key_cache.reshape(batch_count, position_range, KEY_VALUE_HEADS, HEAD_SIZE)
    value_rows = value_cache.reshape(batch_count, position_range, KEY_VALUE_HEADS, HEAD_SIZE)
    scores = (
        jnp.einsum("bgjd,bpgd->bgjp", grouped_query, key_rows, preferred_element_type=jnp.float32)
        * inv
    )
    place = lax.axis_index("tp") * position_range + jnp.arange(position_range, dtype=jnp.int32)
    valid = (place[None, :] < lengths[:, None])[:, None, None, :]
    block_max = jnp.max(jnp.where(valid, scores, -1e30), axis=-1)
    weights = jnp.where(valid, jnp.exp(scores - block_max[..., None]), 0.0)
    block_sum = jnp.sum(weights, axis=-1)
    block_out = jnp.einsum(
        "bgjp,bpgd->bgjd",
        weights.astype(jnp.bfloat16),
        value_rows,
        preferred_element_type=jnp.float32,
    )
    block_max = block_max.reshape(batch_count, QUERY_HEADS)
    block_sum = block_sum.reshape(batch_count, QUERY_HEADS)
    block_out = block_out.reshape(batch_count, QUERY_HEADS, HEAD_SIZE)
    head_start = lax.axis_index("tp") * own_heads
    top_all, total_all, summed_all = combined_all(
        (block_max, block_sum, block_out), "tp", join_parts
    )
    top = lax.dynamic_slice_in_dim(top_all, head_start, own_heads, 1)
    total = lax.dynamic_slice_in_dim(total_all, head_start, own_heads, 1)
    summed = lax.dynamic_slice_in_dim(summed_all, head_start, own_heads, 1)
    query_f = grouped_query.astype(jnp.float32)
    score_new = (jnp.einsum("bgjd,bgd->bgj", query_f, latest_key) * inv).reshape(
        batch_count, QUERY_HEADS
    )
    widened_value = jnp.broadcast_to(
        latest_value[:, :, None, :], (batch_count, KEY_VALUE_HEADS, group_count, HEAD_SIZE)
    ).reshape(batch_count, QUERY_HEADS, HEAD_SIZE)
    score_own = lax.dynamic_slice_in_dim(score_new, head_start, own_heads, 1)
    value_own = lax.dynamic_slice_in_dim(widened_value, head_start, own_heads, 1)
    top_new = jnp.maximum(top, score_own)
    keep = jnp.exp(top - top_new)
    fresh = jnp.exp(score_own - top_new)
    total = total * keep + fresh
    summed = summed * keep[..., None] + fresh[..., None] * value_own
    att = (
        (summed / total[..., None]).reshape(batch_count, own_heads * HEAD_SIZE).astype(jnp.bfloat16)
    )
    partial_value = jnp.dot(att, w_out, preferred_element_type=jnp.float32)
    attn_out = lax.psum_scatter(partial_value, "tp", scatter_dimension=1, tiled=True).astype(
        jnp.bfloat16
    )
    return (attn_out, token_scale)


def solution(mesh):
    placed = (
        P("replica", "tp"),
        P("tp"),
        P(None, "tp"),
        P("tp", None),
        P("replica", "tp", None),
        P("replica", "tp", None),
        P("replica"),
        P("replica"),
    )
    return jax.shard_map(
        on_device,
        mesh=mesh,
        in_specs=placed,
        out_specs=(P("replica", "tp"), P("replica")),
        check_vma=False,
    )
```

profile of v0, /device:TPU:0, one launch (start us, length us, event | category | flops | bytes accessed | tf_op | source)
XLA Modules:
  0.0 267.5 jit_solution(2351034076785041005)
XLA Ops:
  7.2 0.0 copy-start
  7.2 0.0 copy-start.3
  7.2 0.0 copy-start.1
  7.2 0.0 all-gather.5.cloned.1.call-start
  7.3 0.7 convert_element_type.38
  8.0 0.7 convert_element_type.35
  8.7 1.2 dynamic-slice
  10.5 0.8 fusion.22
  11.4 0.2 dynamic-update-slice.1
  11.6 0.2 dynamic-update-slice
  11.8 34.9 %all-reduce.2 = (f32[64]{0:T(128)S(1)}, f32[64]{0:T(128)S(1)}) all-reduce(f32[64]{0:T(128)S(1)} %dynamic-update-slice, f32[64]{0:T(128)S(1)} %dynamic-update-slice.1), channel_id=2, replica_groups=mesh['replica'=2,'tp'=16] {'tp'}, use_global_device_ids=true, to_apply=%add | all-reduce | flops 128 | bytes 1024
  46.7 0.1 slice.70
  46.8 0.1 slice.71
  46.9 0.1 reshape.144
  47.0 0.1 reshape.143
  47.1 0.5 while.26
  47.6 0.0 copy-start.2
  47.6 0.8 fusion.24
  48.4 17.5 %all_gather.31 = bf16[4,16384]{1,0:T(4,128)(2,1)S(1)} all-gather(bf16[4,1024]{1,0:T(4,128)(2,1)S(1)} %fusion.24), channel_id=1, replica_groups=mesh['replica'=2,'tp'=16] {'tp'}, dimensions={1}, use_global_device_ids=true | all-gather | bytes 139264 | tf_op jit(solution)/shard_map/all_gather | solution.py:65
  65.9 8.9 %fusion.8 = bf16[1,576,4]{1,2,0:T(4,128)(2,1)S(1)} fusion(bf16[4,16384]{1,0:T(4,128)(2,1)S(1)} %all_gather.31, bf16[16384,576]{0,1:T(8,128)(2,1)} %param.14, f32[4]{0:T(128)S(1)} %get-tuple-element.120), kind=kOutput, calls=%fused_computation.18 | convolution fusion | flops 75502080 | bytes 19010064 | tf_op jit(solution)/shard_map/dot_general | solution.py:64
  74.8 19.3 %all-gather.2 = bf16[16,576,4]{1,2,0:T(4,128)(2,1)S(1)} all-gather(bf16[1,576,4]{1,2,0:T(4,128)(2,1)S(1)} %fusion.8), channel_id=1, replica_groups=mesh['replica'=2,'tp'=16] {'tp'}, dimensions={0}, use_global_device_ids=true | all-gather | bytes 78336 | tf_op jit(solution)/shard_map/all_gather | solution.py:68
  94.1 0.1 reshape.152
  94.3 0.0 copy-done.3
  94.3 0.1 broadcast_compare_fusion
  94.3 0.1 multiply_cosine_fusion
  94.4 0.1 subtract_convert_fusion
  94.6 0.5 select_reduce_fusion
  95.1 1.0 fusion.9
  96.1 0.0 all-gather.5.cloned.1.call-update
  96.1 0.0 reduce-scatter.4.cloned.1.call-start
  96.1 0.1 all_gather_reshape.9
  96.3 0.1 multiply_subtract_fusion
  96.3 0.1 pad_maximum_fusion.3
  96.4 0.2 fusion.26
  96.7 0.1 reshape.130
  96.7 0.2 fusion.15
  97.0 0.1 all_gather_reshape.10
  97.0 17.6 %all_gather.34 = f32[16,4,64]{2,1,0:T(4,128)S(1)} all-gather(f32[1,4,64]{2,1,0:T(4,128)S(1)} %all_gather_reshape.10), channel_id=1, replica_groups=mesh['replica'=2,'tp'=16] {'tp'}, dimensions={0}, use_global_device_ids=true | all-gather | bytes 17408 | tf_op jit(solution)/shard_map/all_gather | solution.py:12
  114.6 19.2 %all_gather.33 = f32[16,4,64]{2,1,0:T(4,128)S(1)} all-gather(f32[1,4,64]{2,1,0:T(4,128)S(1)} %all_gather_reshape.9), channel_id=1, replica_groups=mesh['replica'=2,'tp'=16] {'tp'}, dimensions={0}, use_global_device_ids=true | all-gather | bytes 17408 | tf_op jit(solution)/shard_map/all_gather | solution.py:12
  133.9 1.2 all-gather.5.cloned.1.call-done
  135.1 0.9 slice_bitcast_fusion
  136.0 1.7 slice.80
  137.7 3.2 %while.27 = (s32[]{:T(128)}, f32[4,64]{1,0:T(4,128)S(1)}, f32[4,64]{1,0:T(4,128)S(1)}, f32[4,64,128]{2,1,0:T(8,128)S(1)}, f32[15,4,64]{2,1,0:T(4,128)S(1)}, /*in...) while((s32[]{:T(128)}, f32[4,64]{1,0:T(4,128)S(1)}, f32[4,64]{1,0:T(4,128)S(1)}, ...), condition=%wide.region_7.8_spmd, body=%wide.region_6.7_spmd.sunk | while | flops 99842 | bytes 403557 | solution.py:15
  137.7 0.2 fusion.50
  137.9 0.2 fusion.50
  138.1 0.2 fusion.50
  138.4 0.2 fusion.50
  138.6 0.2 fusion.50
  138.8 0.2 fusion.50
  139.0 0.2 fusion.50
  139.2 0.2 fusion.50
  139.4 0.2 fusion.50
  139.6 0.2 fusion.50
  139.8 0.2 fusion.50
  140.1 0.2 fusion.50
  140.3 0.2 fusion.50
  140.5 0.2 fusion.50
  140.7 0.2 fusion.50
  140.9 0.1 multiply_add_fusion.1
  141.0 0.1 fusion.30
  141.1 15.6 %convolution_bitcast_fusion = f32[16384,4]{1,0:T(8,128)} fusion(bf16[512,16384]{1,0:T(8,128)(2,1)} %param.15, bf16[1,4,4,128]{3,2,1,0:T(4,128)(2,1)S(1)} %fusion.30), kind=kOutput, calls=%fused_computation.14 | convolution fusion | flops 67108864 | bytes 17043456
  156.7 0.0 reduce-scatter.4.cloned.1.call-update
  156.7 102.1 %reduce-scatter.4.cloned.1.call-done = f32[1024,4]{1,0:T(8,128)} async-done(((f32[16384,4]{1,0:T(8,128)}), f32[1024,4]{1,0:T(8,128)}) %reduce-scatter.4.cloned.1.call-update) | async-done | bytes 16400
  258.8 1.8 copy.21
  (50 shorter events, 0.8 us)
Async XLA Ops:
  7.2 87.4 %copy-start = (bf16[4,128,512]{2,1,0:T(8,128)(2,1)S(1)}, bf16[4,128,512]{2,1,0:T(8,128)(2,1)}, u32[]{:S(2)}) copy-start(bf16[4,128,512]{2,1,0:T(8,128)(2,1)} %param.16) | copy-start | bytes 1572868
  7.2 87.1 %copy-start.3 = (s32[4]{0:T(128)S(1)}, s32[4]{0:T(128)}, u32[]{:S(2)}) copy-start(s32[4]{0:T(128)} %param.18) | copy-start | bytes 52
  7.2 87.9 %copy-start.1 = (bf16[4,128,512]{2,1,0:T(8,128)(2,1)S(1)}, bf16[4,128,512]{2,1,0:T(8,128)(2,1)}, u32[]{:S(2)}) copy-start(bf16[4,128,512]{2,1,0:T(8,128)(2,1)} %param.17) | copy-start | bytes 1572868
  7.2 127.9 %all-gather.5.cloned.1.call-start = ((), (), s32[]{:S(2)}) async-start(), calls=%async_computation.1 | async-start | bytes 2228224 | tf_op jit(solution)/shard_map/all_gather | solution.py:12
  47.6 109.1 %copy-start.2 = (f32[4]{0:T(128)}, f32[4]{0:T(128)S(1)}, u32[]{:S(2)}) copy-start(f32[4]{0:T(128)S(1)} %get-tuple-element.120) | copy-start | bytes 52
  96.1 162.7 %reduce-scatter.4.cloned.1.call-start = ((), (), s32[]{:S(2)}) async-start(), calls=%async_computation.2 | async-start | bytes 8912896
Sparse Core Ops, SparseCore 0:
  96.2 38.8 all-gather.4
  156.8 101.9 reduce-scatter.3
where the time goes:
time: 268 us; the launch traced here: 267 us
  blocking collectives  108 us (40%)
  waiting for transfers between devices  103 us (38%)
  matrix products  26.2 us (10%)
  between operations  14.8 us (6%)
  other arithmetic  7.09 us (3%)
  local copies, waits for them, and re-layouts  6.9 us (3%)
    unnamed x3, waiting for transfers between devices  102 us
    all_gather x2, blocking collectives, combined_all(): pieces = jax.tree.map(lambda part: lax.all_gather(part, axis), value)  36.8 us
    unnamed x1, blocking collectives  34.9 us
    all_gather x1, blocking collectives, on_device(): query_key_value = lax.all_gather(local_proj, 'tp', axis=1, tiled=True)  19.3 us
    all_gather x1, blocking collectives, on_device(): lax.all_gather(quant, 'tp', axis=1, tiled=True)  17.5 us
    unnamed x1, matrix products  15.6 us
    dot_general x1, matrix products, on_device(): jnp.dot(lax.all_gather(quant, 'tp', axis=1, tiled=True), w_qkv, preferred...  8.9 us
  transfers between devices with their start and end apart: 2, of which 2 were waited for; matrix products, arithmetic and copies ran while one was open for 0% of the time, Pallas kernels for 0%

commit v1 on v0

v1 whole, which is shorter than its diff:
```python
import functools

import jax
import jax.numpy as jnp
import numpy as np
from jax import lax
from jax.experimental import pallas as pl
from jax.experimental.pallas import tpu as pltpu
from jax.sharding import PartitionSpec as P

QUERY_HEADS = 64
KEY_VALUE_HEADS = 4
HEAD_SIZE = 128
LANES = 128


def rounded_up(value, step):
    return (value + step - 1) // step * step


def kernel(
    n,
    hidden_hbm,
    gain_hbm,
    wq_hbm,
    wo_hbm,
    key_hbm,
    value_hbm,
    lens_ref,
    pos_ref,
    freq_ref,
    out_ref,
    scale_ref,
    xg,
    gg,
    gained,
    quant,
    wq,
    wo,
    kv,
    vv,
    qg,
    heads,
    so,
    og,
    rs_send,
    rs_recv,
    x_local,
    g_local,
    wq_sem,
    wo_sem,
    kv_sem,
    x_send,
    x_recv,
    g_send,
    g_recv,
    q_send,
    q_recv,
    o_send,
    o_recv,
    r_send,
    r_recv,
):
    me = lax.axis_index("tp")
    batch, dx = hidden_hbm.shape
    width = wq_hbm.shape[0]
    cw = wq_hbm.shape[1]
    padded = qg.shape[2]
    own_rows = og.shape[1]
    own_heads = own_rows // batch
    positions = key_hbm.shape[1]
    group = QUERY_HEADS // KEY_VALUE_HEADS
    f32, bf16 = jnp.float32, jnp.bfloat16

    def wq_copy(c):
        return pltpu.make_async_copy(
            wq_hbm.at[pl.ds(pl.multiple_of(c * dx, dx), dx), :], wq.at[c], wq_sem.at[c]
        )

    def wo_copy(c):
        return pltpu.make_async_copy(
            wo_hbm.at[:, pl.ds(pl.multiple_of(c * dx, dx), dx)], wo.at[c], wo_sem.at[c]
        )

    def remote(src, dst, send, recv, peer):
        return pltpu.make_async_remote_copy(
            src_ref=src,
            dst_ref=dst,
            send_sem=send,
            recv_sem=recv,
            device_id={"tp": peer},
            device_id_type=pl.DeviceIdType.MESH,
        )

    def each_peer(act):
        def step(k, carry):
            act(lax.rem(me + k, n))
            return carry

        lax.fori_loop(1, n, step, 0)

    local_x = pltpu.make_async_copy(hidden_hbm, xg.at[me], x_local)
    local_g = pltpu.make_async_copy(gain_hbm, gg.at[me], g_local)
    local_x.start()
    local_g.start()

    barrier = pltpu.get_barrier_semaphore()
    each_peer(
        lambda peer: pl.semaphore_signal(
            barrier, inc=1, device_id={"tp": peer}, device_id_type=pl.DeviceIdType.MESH
        )
    )

    def start_wq(c, carry):
        wq_copy(c).start()
        return carry

    lax.fori_loop(0, n, start_wq, 0)
    copy_k = pltpu.make_async_copy(key_hbm, kv, kv_sem.at[0])
    copy_v = pltpu.make_async_copy(value_hbm, vv, kv_sem.at[1])
    copy_k.start()
    copy_v.start()

    def start_wo(k, carry):
        wo_copy(lax.rem(me + 1 + k, n)).start()
        return carry

    lax.fori_loop(0, n, start_wo, 0)

    row4 = lax.broadcasted_iota(jnp.int32, (8, LANES), 0) % batch
    place = jnp.zeros((8, LANES), f32)
    for b in range(batch):
        place = jnp.where(row4 == b, pos_ref[b].astype(f32), place)
    angle = place * freq_ref[...]
    cosine = jnp.cos(angle)
    sine = jnp.sin(angle)
    lane8 = lax.broadcasted_iota(jnp.int32, (8, LANES), 1)
    sine = jnp.where(lane8 < HEAD_SIZE // 2, -sine, sine)

    local_x.wait()
    local_g.wait()
    pl.semaphore_wait(barrier, n - 1)

    def send_x(peer):
        remote(xg.at[me], xg.at[me], x_send.at[peer], x_recv.at[me], peer).start()
        remote(gg.at[me], gg.at[me], g_send.at[peer], g_recv.at[me], peer).start()

    each_peer(send_x)

    def gain_piece(s, squares, peak):
        for j in range(dx // LANES):
            x = xg[s, :, j * LANES : (j + 1) * LANES].astype(f32)
            g = gg[s, j : j + 1, :].astype(f32)
            squares = squares + x * x
            y = x * g
            gained[s, :, j * LANES : (j + 1) * LANES] = y
            peak = jnp.maximum(peak, jnp.abs(y))
        return squares, peak

    zero = jnp.zeros((batch, LANES), f32)
    squares, peak = gain_piece(me, zero, zero)

    def take_x(k, carry):
        s = lax.rem(me + k, n)
        remote(xg.at[s], xg.at[s], x_send.at[s], x_recv.at[s], s).wait_recv()
        remote(gg.at[s], gg.at[s], g_send.at[s], g_recv.at[s], s).wait_recv()
        return gain_piece(s, *carry)

    squares, peak = lax.fori_loop(1, n, take_x, (squares, peak))
    rstd = lax.rsqrt(jnp.sum(squares, axis=-1, keepdims=True) / width + 1e-05)
    token_scale = (jnp.max(peak, axis=-1, keepdims=True) * rstd + 1e-06) / 448.0
    for b in range(batch):
        scale_ref[b] = jnp.max(token_scale[b : b + 1, :])

    per = 4 if n % 4 == 0 else 1

    def project(i, acc):
        for u in range(per):
            c = i * per + u
            wq_copy(c).wait()
            quant[c] = (gained[c] * rstd / token_scale).astype(bf16)
        for u in range(per):
            c = i * per + u
            acc = acc + jnp.dot(quant[c], wq[c], preferred_element_type=f32)
        return acc

    acc = lax.fori_loop(0, n // per, project, jnp.zeros((batch, cw), f32))
    proj = (acc * token_scale).astype(bf16).astype(f32)
    if padded > cw:
        proj = jnp.concatenate([proj, jnp.zeros((batch, padded - cw), f32)], axis=1)
    if cw % LANES:
        proj = pltpu.roll(proj, lax.rem(me * cw, LANES), 1)
    qg[me] = proj.astype(bf16)
    each_peer(
        lambda peer: remote(
            qg.at[me], qg.at[me], q_send.at[peer], q_recv.at[me], peer
        ).start()
    )
    each_peer(lambda s: remote(qg.at[s], qg.at[s], q_send.at[s], q_recv.at[s], s).wait_recv())

    total_heads = QUERY_HEADS + 2 * KEY_VALUE_HEADS
    for h in range(total_heads):
        piece = None
        for d in range(h * LANES // cw, (h * LANES + LANES - 1) // cw + 1):
            block = h - d * cw // LANES
            part = qg[d, :, block * LANES : (block + 1) * LANES].astype(f32)
            piece = part if piece is None else piece + part
        heads[h * batch : (h + 1) * batch, :] = piece

    def rotated(rows):
        count = rows.shape[0]
        turned = pltpu.roll(rows, HEAD_SIZE // 2, 1)
        return rows * jnp.tile(cosine, (count // 8, 1)) + turned * jnp.tile(sine, (count // 8, 1))

    copy_k.wait()
    copy_v.wait()
    inv = 1.0 / HEAD_SIZE**0.5
    rows_g = group * batch
    cols = batch * positions
    col = lax.broadcasted_iota(jnp.int32, (8, cols), 1)
    row = lax.broadcasted_iota(jnp.int32, (8, cols), 0)
    limit = jnp.zeros((8, cols), jnp.int32)
    for b in range(batch):
        limit = jnp.where(col // positions == b, lens_ref[b], limit)
    valid8 = (row % batch == col // positions) & (me * positions + col % positions < limit)
    bias8 = jnp.where(valid8, 0.0, -1e30)
    bias = jnp.tile(bias8, (rows_g // 8, 1))
    valid = bias == 0.0
    fresh_rows = rotated(
        heads[QUERY_HEADS * batch : (QUERY_HEADS + KEY_VALUE_HEADS) * batch, :]
    )
    lane = lax.broadcasted_iota(jnp.int32, (rows_g, LANES), 1)
    for g in range(KEY_VALUE_HEADS):
        q = rotated(heads[g * rows_g : (g + 1) * rows_g, :]).astype(bf16)
        k_rows = kv[:, :, g * HEAD_SIZE : (g + 1) * HEAD_SIZE].reshape(cols, HEAD_SIZE)
        v_rows = vv[:, :, g * HEAD_SIZE : (g + 1) * HEAD_SIZE].reshape(cols, HEAD_SIZE)
        s = (
            lax.dot_general(q, k_rows, (((1,), (1,)), ((), ())), preferred_element_type=f32) * inv
        )
        top = jnp.max(jnp.where(valid, s, -1e30), axis=-1, keepdims=True)
        w = jnp.where(valid, jnp.exp(s - top), 0.0)
        total = jnp.sum(w, axis=-1, keepdims=True)
        o = jnp.dot(w.astype(bf16), v_rows, preferred_element_type=f32)
        k_new = fresh_rows[g * batch : (g + 1) * batch, :]
        base = (QUERY_HEADS + KEY_VALUE_HEADS + g) * batch
        v_new = heads[base : base + batch, :]
        s_new = (
            jnp.sum(q.astype(f32) * jnp.tile(k_new, (group, 1)), axis=-1, keepdims=True) * inv
        )
        s_new = jnp.where(me == 0, s_new, -1e30)
        top_new = jnp.maximum(top, s_new)
        keep = jnp.exp(top - top_new)
        fresh = jnp.where(me == 0, jnp.exp(s_new - top_new), 0.0)
        total = total * keep + fresh
        o = o * keep + fresh * jnp.tile(v_new, (group, 1))
        some = total > 0.0
        safe = jnp.where(some, total, 1.0)
        o = o / safe
        lse = jnp.where(some, top_new + jnp.log(safe), -1e30)
        hi = lse.astype(bf16).astype(f32)
        rest = lse - hi
        mid = rest.astype(bf16).astype(f32)
        low = rest - mid
        tail = jnp.where(
            lane == 0, hi, jnp.where(lane == 1, mid, jnp.where(lane == 2, low, 0.0))
        )
        both = jnp.concatenate([o, tail], axis=1).astype(bf16)
        for j in range(group // own_heads):
            so[g * (group // own_heads) + j] = both[j * own_rows : (j + 1) * own_rows, :]

    each_peer(
        lambda peer: remote(
            so.at[peer], og.at[me], o_send.at[peer], o_recv.at[me], peer
        ).start()
    )
    og[me] = so[me]
    each_peer(lambda s: remote(so.at[s], og.at[s], o_send.at[s], o_recv.at[s], s).wait_recv())

    lses = [
        jnp.sum(og[s, :, LANES : 2 * LANES].astype(f32), axis=-1, keepdims=True) for s in range(n)
    ]
    best = functools.reduce(jnp.maximum, lses)
    den = jnp.zeros_like(best)
    num = jnp.zeros((own_rows, LANES), f32)
    for s in range(n):
        share = jnp.exp(lses[s] - best)
        den = den + share
        num = num + share * og[s, :, 0:LANES].astype(f32)
    att = num / den
    att = jnp.concatenate(
        [att[j * batch : (j + 1) * batch, :] for j in range(own_heads)], axis=1
    ).astype(bf16)

    def project_out(k, carry):
        e = lax.rem(me + 1 + k, n)
        wo_copy(e).wait()
        rs_send[e] = jnp.dot(att, wo[e], preferred_element_type=f32).astype(bf16)
        remote(rs_send.at[e], rs_recv.at[me], r_send.at[e], r_recv.at[me], e).start()
        return carry

    lax.fori_loop(0, n - 1, project_out, 0)
    wo_copy(me).wait()
    own = jnp.dot(att, wo[me], preferred_element_type=f32)

    def take_r(k, carry):
        s = lax.rem(me + k, n)
        remote(rs_send.at[s], rs_recv.at[s], r_send.at[s], r_recv.at[s], s).wait_recv()
        return carry + rs_recv[s].astype(f32)

    out_ref[...] = lax.fori_loop(1, n, take_r, own).astype(bf16)

    def finish(peer):
        remote(xg.at[me], xg.at[me], x_send.at[peer], x_recv.at[me], peer).wait_send()
        remote(gg.at[me], gg.at[me], g_send.at[peer], g_recv.at[me], peer).wait_send()
        remote(qg.at[me], qg.at[me], q_send.at[peer], q_recv.at[me], peer).wait_send()
        remote(so.at[peer], og.at[me], o_send.at[peer], o_recv.at[me], peer).wait_send()
        remote(rs_send.at[peer], rs_recv.at[me], r_send.at[peer], r_recv.at[me], peer).wait_send()

    each_peer(finish)


def on_device(n, hidden_in, norm_gain, w_qkv, w_out, key_cache, value_cache, lengths, positions):
    batch, dx = hidden_in.shape
    width, cw = w_qkv.shape
    own_rows = w_out.shape[0] // HEAD_SIZE * batch
    total_heads = QUERY_HEADS + 2 * KEY_VALUE_HEADS
    widest = max(d * cw % LANES for d in range(n)) + cw
    padded = rounded_up(widest, LANES)
    half = HEAD_SIZE // 2
    freq = np.float32(500000.0) ** (
        -(np.arange(half, dtype=np.float32) * np.float32(2.0)) / np.float32(HEAD_SIZE)
    )
    freq = jnp.asarray(np.tile(freq.astype(np.float32), 2)[None, :])
    bf16, f32 = jnp.bfloat16, jnp.float32
    dma = pltpu.SemaphoreType.DMA
    hbm = pl.BlockSpec(memory_space=pl.ANY)
    smem = pl.BlockSpec(memory_space=pltpu.SMEM)
    vmem = pl.BlockSpec(memory_space=pltpu.VMEM)
    return pl.pallas_call(
        functools.partial(kernel, n),
        out_shape=(
            jax.ShapeDtypeStruct((batch, dx), bf16),
            jax.ShapeDtypeStruct((batch,), f32),
        ),
        in_specs=[hbm] * 6 + [smem, smem, vmem],
        out_specs=(vmem, smem),
        scratch_shapes=[
            pltpu.VMEM((n, batch, dx), bf16),
            pltpu.VMEM((n, dx // LANES, LANES), bf16),
            pltpu.VMEM((n, batch, dx), f32),
            pltpu.VMEM((n, batch, dx), bf16),
            pltpu.VMEM((n, dx, cw), bf16),
            pltpu.VMEM((n, w_out.shape[0], dx), bf16),
            pltpu.VMEM(key_cache.shape, bf16),
            pltpu.VMEM(value_cache.shape, bf16),
            pltpu.VMEM((n, batch, padded), bf16),
            pltpu.VMEM((total_heads * batch, HEAD_SIZE), f32),
            pltpu.VMEM((n, own_rows, 2 * LANES), bf16),
            pltpu.VMEM((n, own_rows, 2 * LANES), bf16),
            pltpu.VMEM((n, batch, dx), bf16),
            pltpu.VMEM((n, batch, dx), bf16),
            dma(()),
            dma(()),
            dma((n,)),
            dma((n,)),
            dma((2,)),
        ]
        + [dma((n,))] * 10,
        compiler_params=pltpu.CompilerParams(
            collective_id=0, has_side_effects=True, vmem_limit_bytes=60 * 1024 * 1024
        ),
        name="decode",
    )(
        hidden_in,
        norm_gain.reshape(dx // LANES, LANES),
        w_qkv,
        w_out,
        key_cache,
        value_cache,
        lengths,
        positions,
        freq,
    )


def solution(mesh):
    placed = (
        P("replica", "tp"),
        P("tp"),
        P(None, "tp"),
        P("tp", None),
        P("replica", "tp", None),
        P("replica", "tp", None),
        P("replica"),
        P("replica"),
    )
    return jax.shard_map(
        functools.partial(on_device, mesh.shape["tp"]),
        mesh=mesh,
        in_specs=placed,
        out_specs=(P("replica", "tp"), P("replica")),
        check_vma=False,
    )
```

time: 268 us -> 66.1 us (0.25)
  blocking collectives: 108 us -> 0 us
  waiting for transfers between devices: 103 us -> 0 us
  Pallas kernels: 0 us -> 35.8 us
  matrix products: 26.2 us -> 0 us
  local copies, waits for them, and re-layouts: 6.9 us -> 28.9 us
  between operations: 14.8 us -> 0.64 us
  other arithmetic: 7.09 us -> 0 us
    unnamed x3 -> x0, waiting for transfers between devices: 102 us -> none
    all_gather x4 -> x0, blocking collectives: 73.6 us -> none  [the longest x2 36.8 us: combined_all(): pieces = jax.tree.map(lambda part: lax.all_gather(part, axis), value)]
    pallas_call x0 -> x1, Pallas kernels: none -> 35.8 us  [on_device(): pl.pallas_call(functools.partial(kernel, n), out_shape=(jax.ShapeDtypeStr...]
    unnamed x1 -> x0, blocking collectives: 34.9 us -> none
    unnamed x16 -> x3, local copies, waits for them, and re-layouts: 3.69 us -> 28.9 us
    unnamed x1 -> x0, matrix products: 15.6 us -> none
    dot_general x4 -> x0, matrix products: 10.6 us -> none  [the longest x1 8.9 us: on_device(): jnp.dot(lax.all_gather(quant, 'tp', axis=1, tiled=True), w_qkv, preferred...]
    add x47 -> x0, other arithmetic: 3.24 us -> none  [the longest x15 2.46 us: join_parts(): summed = left[2] * scale_left[..., None] + right[2] * scale_right[..., None]]
  transfers between devices with their start and end apart: 2 -> 0, of which waited for: 2 -> 0; matrix products, arithmetic and copies ran while one was open for 0% -> 0% of each run, Pallas kernels for 0% -> 0%
where the time goes in v1:
time: 66.1 us; the launch traced here: 65.3 us
  Pallas kernels  35.8 us (54%)
  local copies, waits for them, and re-layouts  28.9 us (44%)
    pallas_call x1, Pallas kernels, on_device(): pl.pallas_call(functools.partial(kernel, n), out_shape=(jax.ShapeDtypeStr...  35.8 us
    unnamed x3, local copies, waits for them, and re-layouts  28.9 us

profile of v1, /device:TPU:0, one launch (start us, length us, event | category | flops | bytes accessed | tf_op | source)
XLA Modules:
  0.0 65.3 jit_solution(17546508489970328129)
XLA Ops:
  0.6 26.5 %copy.11.wq_hbm = bf16[16384,576]{1,0:T(8,128)(2,1)} copy(bf16[16384,576]{0,1:T(8,128)(2,1)} %param.11) | data formatting | bytes 37748736 | tf_op args[2]
  27.1 35.8 %decode.1 = (bf16[4,1024]{1,0:T(4,128)(2,1)}, f32[4]{0:T(128)}) custom-call(bf16[4,1024]{1,0:T(4,128)(2,1)} %hidden_hbm.1, bf16[8,128]{1,0:T(8,128)(2,1)} %bitcast.1, bf16[16384,576]{1,0:T(8,128)(2,1)} %copy.11.wq_hbm, bf16[512,16384]{1,0:T(8,128)(2,1)} %wo_hbm.1, bf16[4,128,512]{2,1,0:T(8,128)(2,1)} %key_hbm.1, bf16[4,128,512]{2,1,0:T(8,128)(2,1)} %value_hbm.1, ...), custom_call_target="tpu_custom_call" | custom-call | tf_op jit(solution)/shard_map/decode/pallas_call | solution.py:339
  62.9 1.3 %copy.14 = bf16[4,1024]{1,0:T(4,128)(2,1)} copy(bf16[4,1024]{1,0:T(4,128)(2,1)} %get-tuple-element.4) | data formatting | bytes 16384
  64.2 1.1 %copy.15 = f32[4]{0:T(128)} copy(f32[4]{0:T(128)} %get-tuple-element.5) | data formatting | bytes 32

commit v2 on v1

--- a/solution.py
+++ b/solution.py
@@ -63,8 +63,7 @@
 ):
     me = lax.axis_index("tp")
     batch, dx = hidden_hbm.shape
-    width = wq_hbm.shape[0]
-    cw = wq_hbm.shape[1]
+    cw, width = wq_hbm.shape
     padded = qg.shape[2]
     own_rows = og.shape[1]
     own_heads = own_rows // batch
@@ -73,9 +72,8 @@
     f32, bf16 = jnp.float32, jnp.bfloat16
 
     def wq_copy(c):
-        return pltpu.make_async_copy(
-            wq_hbm.at[pl.ds(pl.multiple_of(c * dx, dx), dx), :], wq.at[c], wq_sem.at[c]
-        )
+        span = pl.ds(pl.multiple_of(c * dx, dx), dx)
+        return pltpu.make_async_copy(wq_hbm.at[:, span], wq.at[:, span], wq_sem.at[c])
 
     def wo_copy(c):
         return pltpu.make_async_copy(
@@ -126,6 +124,16 @@
         return carry
 
     lax.fori_loop(0, n, start_wo, 0)
+
+    local_x.wait()
+    local_g.wait()
+    pl.semaphore_wait(barrier, n - 1)
+
+    def send_x(peer):
+        remote(xg.at[me], xg.at[me], x_send.at[peer], x_recv.at[me], peer).start()
+        remote(gg.at[me], gg.at[me], g_send.at[peer], g_recv.at[me], peer).start()
+
+    each_peer(send_x)
 
     row4 = lax.broadcasted_iota(jnp.int32, (8, LANES), 0) % batch
     place = jnp.zeros((8, LANES), f32)
@@ -137,16 +145,6 @@
     lane8 = lax.broadcasted_iota(jnp.int32, (8, LANES), 1)
     sine = jnp.where(lane8 < HEAD_SIZE // 2, -sine, sine)
 
-    local_x.wait()
-    local_g.wait()
-    pl.semaphore_wait(barrier, n - 1)
-
-    def send_x(peer):
-        remote(xg.at[me], xg.at[me], x_send.at[peer], x_recv.at[me], peer).start()
-        remote(gg.at[me], gg.at[me], g_send.at[peer], g_recv.at[me], peer).start()
-
-    each_peer(send_x)
-
     def gain_piece(s, squares, peak):
         for j in range(dx // LANES):
             x = xg[s, :, j * LANES : (j + 1) * LANES].astype(f32)
@@ -178,14 +176,15 @@
         for u in range(per):
             c = i * per + u
             wq_copy(c).wait()
-            quant[c] = (gained[c] * rstd / token_scale).astype(bf16)
-        for u in range(per):
-            c = i * per + u
-            acc = acc + jnp.dot(quant[c], wq[c], preferred_element_type=f32)
-        return acc
-
-    acc = lax.fori_loop(0, n // per, project, jnp.zeros((batch, cw), f32))
-    proj = (acc * token_scale).astype(bf16).astype(f32)
+            span = pl.ds(pl.multiple_of(c * dx, dx), dx)
+            quant[:, span] = (gained[c] * rstd / token_scale).astype(bf16)
+        span = pl.ds(pl.multiple_of(i * per * dx, per * dx), per * dx)
+        return acc + lax.dot_general(
+            wq[:, span], quant[:, span], (((1,), (1,)), ((), ())), preferred_element_type=f32
+        )
+
+    acc = lax.fori_loop(0, n // per, project, jnp.zeros((cw, batch), f32))
+    proj = (acc.T * token_scale).astype(bf16).astype(f32)
     if padded > cw:
         proj = jnp.concatenate([proj, jnp.zeros((batch, padded - cw), f32)], axis=1)
     if cw % LANES:
@@ -321,7 +320,7 @@
 
 def on_device(n, hidden_in, norm_gain, w_qkv, w_out, key_cache, value_cache, lengths, positions):
     batch, dx = hidden_in.shape
-    width, cw = w_qkv.shape
+    cw = w_qkv.shape[1]
     own_rows = w_out.shape[0] // HEAD_SIZE * batch
     total_heads = QUERY_HEADS + 2 * KEY_VALUE_HEADS
     widest = max(d * cw % LANES for d in range(n)) + cw
@@ -348,8 +347,8 @@
             pltpu.VMEM((n, batch, dx), bf16),
             pltpu.VMEM((n, dx // LANES, LANES), bf16),
             pltpu.VMEM((n, batch, dx), f32),
-            pltpu.VMEM((n, batch, dx), bf16),
-            pltpu.VMEM((n, dx, cw), bf16),
+            pltpu.VMEM((batch, n * dx), bf16),
+            pltpu.VMEM((cw, n * dx), bf16),
             pltpu.VMEM((n, w_out.shape[0], dx), bf16),
             pltpu.VMEM(key_cache.shape, bf16),
             pltpu.VMEM(value_cache.shape, bf16),
@@ -373,7 +372,7 @@
     )(
         hidden_in,
         norm_gain.reshape(dx // LANES, LANES),
-        w_qkv,
+        w_qkv.T,
         w_out,
         key_cache,
         value_cache,

time: 66.1 us -> 41.7 us (0.63)
  local copies, waits for them, and re-layouts: 28.9 us -> 2.44 us
  Pallas kernels: 35.8 us -> 38.3 us
    unnamed x3 -> x2, local copies, waits for them, and re-layouts: 28.9 us -> 2.44 us
    pallas_call x1, Pallas kernels: 35.8 us -> 38.3 us  [on_device(): pl.pallas_call(functools.partial(kernel, n), out_shape=(jax.ShapeDtypeStr...]
where the time goes in v2:
time: 41.7 us; the launch traced here: 41.4 us
  Pallas kernels  38.3 us (92%)
  local copies, waits for them, and re-layouts  2.44 us (6%)
  between operations  0.64 us (2%)
    pallas_call x1, Pallas kernels, on_device(): pl.pallas_call(functools.partial(kernel, n), out_shape=(jax.ShapeDtypeStr...  38.3 us
    unnamed x2, local copies, waits for them, and re-layouts  2.44 us

profile of v2, /device:TPU:0, one launch (start us, length us, event | category | flops | bytes accessed | tf_op | source)
XLA Modules:
  0.0 41.4 jit_solution(8858959414830961037)
XLA Ops:
  0.6 38.3 %decode.1 = (bf16[4,1024]{1,0:T(4,128)(2,1)}, f32[4]{0:T(128)}) custom-call(bf16[4,1024]{1,0:T(4,128)(2,1)} %hidden_hbm.1, bf16[8,128]{1,0:T(8,128)(2,1)} %bitcast.3, bf16[576,16384]{1,0:T(8,128)(2,1)} %bitcast.2, bf16[512,16384]{1,0:T(8,128)(2,1)} %wo_hbm.1, bf16[4,128,512]{2,1,0:T(8,128)(2,1)} %key_hbm.1, bf16[4,128,512]{2,1,0:T(8,128)(2,1)} %value_hbm.1, ...), custom_call_target="tpu_custom_call" | custom-call | tf_op jit(solution)/shard_map/decode/pallas_call | solution.py:338
  38.9 1.3 %copy.13 = bf16[4,1024]{1,0:T(4,128)(2,1)} copy(bf16[4,1024]{1,0:T(4,128)(2,1)} %get-tuple-element.4) | data formatting | bytes 16384
  40.2 1.1 %copy.14 = f32[4]{0:T(128)} copy(f32[4]{0:T(128)} %get-tuple-element.5) | data formatting | bytes 32

commit v3 on v2

--- a/solution.py
+++ b/solution.py
@@ -32,13 +32,13 @@
     out_ref,
     scale_ref,
     xg,
-    gg,
     gained,
     quant,
     wq,
     wo,
     kv,
     vv,
+    stage,
     qg,
     heads,
     so,
@@ -52,8 +52,6 @@
     kv_sem,
     x_send,
     x_recv,
-    g_send,
-    g_recv,
     q_send,
     q_recv,
     o_send,
@@ -62,9 +60,14 @@
     r_recv,
 ):
     me = lax.axis_index("tp")
-    batch, dx = hidden_hbm.shape
+    dx = wo.shape[2]
+    batch = lens_ref.shape[0]
+    pieces = dx // LANES
+    x_rows = pieces * batch
+    gain_at = xg.shape[1] - rounded_up(pieces, 8)
     cw, width = wq_hbm.shape
-    padded = qg.shape[2]
+    blocks = stage.shape[0] // batch
+    padded = blocks * LANES
     own_rows = og.shape[1]
     own_heads = own_rows // batch
     positions = key_hbm.shape[1]
@@ -97,8 +100,8 @@
 
         lax.fori_loop(1, n, step, 0)
 
-    local_x = pltpu.make_async_copy(hidden_hbm, xg.at[me], x_local)
-    local_g = pltpu.make_async_copy(gain_hbm, gg.at[me], g_local)
+    local_x = pltpu.make_async_copy(hidden_hbm, xg.at[me, pl.ds(0, x_rows), :], x_local)
+    local_g = pltpu.make_async_copy(gain_hbm, xg.at[me, pl.ds(gain_at, pieces), :], g_local)
     local_x.start()
     local_g.start()
 
@@ -131,7 +134,6 @@
 
     def send_x(peer):
         remote(xg.at[me], xg.at[me], x_send.at[peer], x_recv.at[me], peer).start()
-        remote(gg.at[me], gg.at[me], g_send.at[peer], g_recv.at[me], peer).start()
 
     each_peer(send_x)
 
@@ -145,28 +147,43 @@
     lane8 = lax.broadcasted_iota(jnp.int32, (8, LANES), 1)
     sine = jnp.where(lane8 < HEAD_SIZE // 2, -sine, sine)
 
+    half8 = lax.broadcasted_iota(jnp.int32, (8, LANES), 0) // batch
+    per8 = 8 // batch
+
     def gain_piece(s, squares, peak):
-        for j in range(dx // LANES):
-            x = xg[s, :, j * LANES : (j + 1) * LANES].astype(f32)
-            g = gg[s, j : j + 1, :].astype(f32)
-            squares = squares + x * x
-            y = x * g
-            gained[s, :, j * LANES : (j + 1) * LANES] = y
+        x = xg[s, 0:x_rows, :].astype(f32)
+        g = xg[s, gain_at : gain_at + rounded_up(pieces, 8), :].astype(f32)
+        for j in range(x_rows // 8):
+            x8 = x[8 * j : 8 * j + 8, :]
+            g8 = jnp.zeros((8, LANES), f32)
+            for u in range(per8):
+                r = j * per8 + u
+                g8 = jnp.where(half8 == u, g[r : r + 1, :], g8)
+            squares = squares + x8 * x8
+            y = x8 * g8
+            gained[s, 8 * j : 8 * j + 8, :] = y
             peak = jnp.maximum(peak, jnp.abs(y))
         return squares, peak
 
-    zero = jnp.zeros((batch, LANES), f32)
+    zero = jnp.zeros((8, LANES), f32)
     squares, peak = gain_piece(me, zero, zero)
 
     def take_x(k, carry):
         s = lax.rem(me + k, n)
         remote(xg.at[s], xg.at[s], x_send.at[s], x_recv.at[s], s).wait_recv()
-        remote(gg.at[s], gg.at[s], g_send.at[s], g_recv.at[s], s).wait_recv()
         return gain_piece(s, *carry)
 
     squares, peak = lax.fori_loop(1, n, take_x, (squares, peak))
+    squares = sum(squares[u * batch : (u + 1) * batch, :] for u in range(per8))
+    peak = functools.reduce(
+        jnp.maximum, [peak[u * batch : (u + 1) * batch, :] for u in range(per8)]
+    )
     rstd = lax.rsqrt(jnp.sum(squares, axis=-1, keepdims=True) / width + 1e-05)
     token_scale = (jnp.max(peak, axis=-1, keepdims=True) * rstd + 1e-06) / 448.0
+    rstd_rows = jnp.tile(jnp.broadcast_to(rstd, (batch, LANES)), (per8, 1))
+    scale_rows = jnp.tile(jnp.broadcast_to(token_scale, (batch, LANES)), (per8, 1))
+    rstd_rows = jnp.tile(rstd_rows, (x_rows // 8, 1))
+    scale_rows = jnp.tile(scale_rows, (x_rows // 8, 1))
     for b in range(batch):
         scale_ref[b] = jnp.max(token_scale[b : b + 1, :])
 
@@ -177,7 +194,10 @@
             c = i * per + u
             wq_copy(c).wait()
             span = pl.ds(pl.multiple_of(c * dx, dx), dx)
-            quant[:, span] = (gained[c] * rstd / token_scale).astype(bf16)
+            rows = gained[c] * rstd_rows / scale_rows
+            quant[:, span] = jnp.concatenate(
+                [rows[j * batch : (j + 1) * batch, :] for j in range(pieces)], axis=1
+            ).astype(bf16)
         span = pl.ds(pl.multiple_of(i * per * dx, per * dx), per * dx)
         return acc + lax.dot_general(
             wq[:, span], quant[:, span], (((1,), (1,)), ((), ())), preferred_element_type=f32
@@ -189,7 +209,9 @@
         proj = jnp.concatenate([proj, jnp.zeros((batch, padded - cw), f32)], axis=1)
     if cw % LANES:
         proj = pltpu.roll(proj, lax.rem(me * cw, LANES), 1)
-    qg[me] = proj.astype(bf16)
+    for j in range(blocks):
+        stage[j * batch : (j + 1) * batch, :] = proj[:, j * LANES : (j + 1) * LANES]
+    qg[me, 0 : blocks * batch, :] = stage[...].astype(bf16)
     each_peer(
         lambda peer: remote(
             qg.at[me], qg.at[me], q_send.at[peer], q_recv.at[me], peer
@@ -198,11 +220,12 @@
     each_peer(lambda s: remote(qg.at[s], qg.at[s], q_send.at[s], q_recv.at[s], s).wait_recv())
 
     total_heads = QUERY_HEADS + 2 * KEY_VALUE_HEADS
+    unpacked = [qg[d].astype(f32) for d in range(n)]
     for h in range(total_heads):
         piece = None
         for d in range(h * LANES // cw, (h * LANES + LANES - 1) // cw + 1):
             block = h - d * cw // LANES
-            part = qg[d, :, block * LANES : (block + 1) * LANES].astype(f32)
+            part = unpacked[d][block * batch : (block + 1) * batch, :]
             piece = part if piece is None else piece + part
         heads[h * batch : (h + 1) * batch, :] = piece
 
@@ -290,16 +313,28 @@
         [att[j * batch : (j + 1) * batch, :] for j in range(own_heads)], axis=1
     ).astype(bf16)
 
-    def project_out(k, carry):
-        e = lax.rem(me + 1 + k, n)
-        wo_copy(e).wait()
-        rs_send[e] = jnp.dot(att, wo[e], preferred_element_type=f32).astype(bf16)
-        remote(rs_send.at[e], rs_recv.at[me], r_send.at[e], r_recv.at[me], e).start()
+    def rows_of(part):
+        return jnp.concatenate(
+            [part[:, j * LANES : (j + 1) * LANES] for j in range(pieces)], axis=0
+        )
+
+    unroll = 3 if (n - 1) % 3 == 0 else 1
+
+    def project_out(i, carry):
+        parts = []
+        for u in range(unroll):
+            e = lax.rem(me + 1 + i * unroll + u, n)
+            wo_copy(e).wait()
+            parts.append(jnp.dot(att, wo[e], preferred_element_type=f32))
+        for u in range(unroll):
+            e = lax.rem(me + 1 + i * unroll + u, n)
+            rs_send[e] = rows_of(parts[u]).astype(bf16)
+            remote(rs_send.at[e], rs_recv.at[me], r_send.at[e], r_recv.at[me], e).start()
         return carry
 
-    lax.fori_loop(0, n - 1, project_out, 0)
+    lax.fori_loop(0, (n - 1) // unroll, project_out, 0)
     wo_copy(me).wait()
-    own = jnp.dot(att, wo[me], preferred_element_type=f32)
+    own = rows_of(jnp.dot(att, wo[me], preferred_element_type=f32))
 
     def take_r(k, carry):
         s = lax.rem(me + k, n)
@@ -310,7 +345,6 @@
 
     def finish(peer):
         remote(xg.at[me], xg.at[me], x_send.at[peer], x_recv.at[me], peer).wait_send()
-        remote(gg.at[me], gg.at[me], g_send.at[peer], g_recv.at[me], peer).wait_send()
         remote(qg.at[me], qg.at[me], q_send.at[peer], q_recv.at[me], peer).wait_send()
         remote(so.at[peer], og.at[me], o_send.at[peer], o_recv.at[me], peer).wait_send()
         remote(rs_send.at[peer], rs_recv.at[me], r_send.at[peer], r_recv.at[me], peer).wait_send()
@@ -324,7 +358,9 @@
     own_rows = w_out.shape[0] // HEAD_SIZE * batch
     total_heads = QUERY_HEADS + 2 * KEY_VALUE_HEADS
     widest = max(d * cw % LANES for d in range(n)) + cw
-    padded = rounded_up(widest, LANES)
+    blocks = rounded_up(widest, LANES) // LANES
+    pieces = dx // LANES
+    x_height = rounded_up(pieces * batch, 8) + rounded_up(pieces, 8)
     half = HEAD_SIZE // 2
     freq = np.float32(500000.0) ** (
         -(np.arange(half, dtype=np.float32) * np.float32(2.0)) / np.float32(HEAD_SIZE)
@@ -335,42 +371,42 @@
     hbm = pl.BlockSpec(memory_space=pl.ANY)
     smem = pl.BlockSpec(memory_space=pltpu.SMEM)
     vmem = pl.BlockSpec(memory_space=pltpu.VMEM)
-    return pl.pallas_call(
+    out, token_scale = pl.pallas_call(
         functools.partial(kernel, n),
         out_shape=(
-            jax.ShapeDtypeStruct((batch, dx), bf16),
+            jax.ShapeDtypeStruct((pieces * batch, LANES), bf16),
             jax.ShapeDtypeStruct((batch,), f32),
         ),
         in_specs=[hbm] * 6 + [smem, smem, vmem],
         out_specs=(vmem, smem),
         scratch_shapes=[
-            pltpu.VMEM((n, batch, dx), bf16),
-            pltpu.VMEM((n, dx // LANES, LANES), bf16),
-            pltpu.VMEM((n, batch, dx), f32),
+            pltpu.VMEM((n, x_height, LANES), bf16),
+            pltpu.VMEM((n, pieces * batch, LANES), f32),
             pltpu.VMEM((batch, n * dx), bf16),
             pltpu.VMEM((cw, n * dx), bf16),
             pltpu.VMEM((n, w_out.shape[0], dx), bf16),
             pltpu.VMEM(key_cache.shape, bf16),
             pltpu.VMEM(value_cache.shape, bf16),
-            pltpu.VMEM((n, batch, padded), bf16),
+            pltpu.VMEM((blocks * batch, LANES), f32),
+            pltpu.VMEM((n, rounded_up(blocks * batch, 8), LANES), bf16),
             pltpu.VMEM((total_heads * batch, HEAD_SIZE), f32),
             pltpu.VMEM((n, own_rows, 2 * LANES), bf16),
             pltpu.VMEM((n, own_rows, 2 * LANES), bf16),
-            pltpu.VMEM((n, batch, dx), bf16),
-            pltpu.VMEM((n, batch, dx), bf16),
+            pltpu.VMEM((n, pieces * batch, LANES), bf16),
+            pltpu.VMEM((n, pieces * batch, LANES), bf16),
             dma(()),
             dma(()),
             dma((n,)),
             dma((n,)),
             dma((2,)),
         ]
-        + [dma((n,))] * 10,
+        + [dma((n,))] * 8,
         compiler_params=pltpu.CompilerParams(
             collective_id=0, has_side_effects=True, vmem_limit_bytes=60 * 1024 * 1024
         ),
         name="decode",
     )(
-        hidden_in,
+        hidden_in.reshape(batch, pieces, LANES).transpose(1, 0, 2).reshape(-1, LANES),
         norm_gain.reshape(dx // LANES, LANES),
         w_qkv.T,
         w_out,
@@ -380,6 +416,8 @@
         positions,
         freq,
     )
+    out = out.reshape(pieces, batch, LANES).transpose(1, 0, 2).reshape(batch, dx)
+    return out, token_scale
 
 
 def solution(mesh):

time: 41.7 us -> 41.6 us (level)
  no operation moved by 1% of the time
where the time goes in v3:
time: 41.6 us; the launch traced here: 41.3 us
  Pallas kernels  38.2 us (92%)
  local copies, waits for them, and re-layouts  2.44 us (6%)
  between operations  0.64 us (2%)
    pallas_call x1, Pallas kernels, on_device(): pl.pallas_call(functools.partial(kernel, n), out_shape=(jax.ShapeDtypeStr...  38.2 us
    unnamed x2, local copies, waits for them, and re-layouts  2.44 us

profile of v3, /device:TPU:0, one launch (start us, length us, event | category | flops | bytes accessed | tf_op | source)
XLA Modules:
  0.0 41.3 jit_solution(11083486205873715954)
XLA Ops:
  0.6 38.2 %decode.1 = (bf16[32,128]{1,0:T(8,128)(2,1)}, f32[4]{0:T(128)}) custom-call(bf16[32,128]{1,0:T(8,128)(2,1)} %bitcast.13, bf16[8,128]{1,0:T(8,128)(2,1)} %bitcast.15, bf16[576,16384]{1,0:T(8,128)(2,1)} %bitcast.12, bf16[512,16384]{1,0:T(8,128)(2,1)} %wo_hbm.1, bf16[4,128,512]{2,1,0:T(8,128)(2,1)} %key_hbm.1, bf16[4,128,512]{2,1,0:T(8,128)(2,1)} %value_hbm.1, ...), custom_call_target="tpu_custom_call" | custom-call | tf_op jit(solution)/shard_map/decode/pallas_call | solution.py:374
  38.8 1.3 %copy.15 = bf16[4,1024]{1,0:T(4,128)(2,1)} copy(bf16[4,1024]{1,0:T(4,128)(2,1)} %bitcast.14) | data formatting | bytes 16384
  40.1 1.1 %copy.16 = f32[4]{0:T(128)} copy(f32[4]{0:T(128)} %get-tuple-element.9) | data formatting | bytes 32
